TPU v7x, 32 devices: a whole 2x2x4 slice. The times are simulated.
32 devices in a mesh: rep: 8 (over z, x), rows: 4 (over y, core).
Axes of the slice: x: 2, y: 2, z: 4, core: 2. Of those that a mesh axis runs over, the one named last changes fastest.
Arguments:
- item_table: bfloat16 [131072, 128], P(('rep', 'rows')), may hold values from -6 to 6
- history_ids: int32 [512, 64], P('rows'), may hold values from 0 to 131071, as said below
- history_mask: int32 [512, 64], P('rows'), may hold values 0 or 1
Outputs:
- user_vectors: float32 [512, 128], P('rows')
Inputs may be any that keep to these rules, and one draw needn't show every extreme that they name: `history_ids`: among the slots of the 128 bags of one index of rows (bags b * 128 to (b + 1) * 128 - 1), exactly 256 ids fall in each block of 4096 consecutive table rows, used or not.
All inputs are finite; a program needn't handle non-finite values. No bound on the sum of `history_mask` on one device may be relied on, other than what follows from the above.
Results may differ from a plain program's by a relative error of at most 0.0017.
Values may be sent and summed in bfloat16 or wider, within the bound.
No kernel may reach another device: no remote copies, remote signals or barrier semaphores. Data moves between devices by JAX's collectives and lax.ppermute only.
A program may use at most 128 MiB of HBM per device.

v0:
```python
import math
import jax
import jax.numpy as jnp
from jax import lax
from jax.sharding import PartitionSpec as P


def pool_rows(ids, mask, piece, offset):
    nbags, length = ids.shape
    block = math.gcd(nbags, 512)
    nhigh = piece.shape[0] // 128
    width = piece.shape[1]
    local = ids - offset
    high = jnp.floor_divide(local, 128)
    low = jnp.remainder(local, 128)

    def one_block(args):
        high_b, low_b, mask_b = args
        high_hot = (high_b[:, :, None] == jnp.arange(nhigh, dtype=jnp.int32)).astype(jnp.bfloat16)
        low_hot = (
            (low_b[:, :, None] == jnp.arange(128, dtype=jnp.int32)) & (mask_b[:, :, None] > 0)
        ).astype(jnp.bfloat16)
        counts = jnp.einsum("blh,blo->bho", high_hot, low_hot, preferred_element_type=jnp.float32)
        counts = counts.astype(jnp.bfloat16).reshape(block, nhigh * 128)
        return jnp.dot(counts, piece, preferred_element_type=jnp.float32)

    shaped = (
        high.reshape(-1, block, length),
        low.reshape(-1, block, length),
        mask.reshape(-1, block, length),
    )
    return lax.map(one_block, shaped).reshape(nbags, width)


def normalize(pooled):
    return pooled / jnp.sqrt(jnp.mean(pooled * pooled, axis=1, keepdims=True) + 1e-06)


def on_device(item_table, history_ids, history_mask):
    rows_dev = item_table.shape[0]
    group_size = lax.axis_size("rows")
    group_rows = rows_dev * group_size
    group_base = lax.axis_index("rep") * group_rows
    partial_value = pool_rows(
        history_ids,
        history_mask,
        lax.all_gather(item_table, "rows", axis=0, tiled=True),
        group_base,
    )
    pooled = lax.psum(partial_value, "rep")
    return normalize(pooled)


def solution(mesh):
    return jax.shard_map(
        on_device,
        mesh=mesh,
        in_specs=(P(("rep", "rows"), None), P("rows", None), P("rows", None)),
        out_specs=P("rows", None),
        check_vma=False,
    )
```

profile of v0, /device:TPU:0, one launch (start us, length us, event | category | flops | bytes accessed | tf_op | source)
XLA Modules:
  0.0 131.9 jit_solution(6185900074222709909)
XLA Ops:
  6.5 0.0 all-gather.2.cloned.1.call-start
  6.5 0.7 all-gather.2.cloned.1.call-update
  7.3 0.0 all-reduce.2.cloned.1.call-start
  7.3 0.8 add_select_fusion.1
  8.1 0.1 copy.4
  8.2 0.1 copy.5
  8.3 0.8 broadcast_compare_fusion
  9.1 0.1 copy.6
  9.2 10.8 %fusion.6 = bf16[128,128,128]{2,1,0:T(8,128)(2,1)} fusion(s32[128,64]{1,0:T(8,128)S(1)} %copy.5, s32[128,64]{1,0:T(8,128)S(1)} %copy.4, pred[128,64]{1,0:T(8,128)(4,1)S(1)} %copy.6), kind=kOutput, calls=%fused_computation.7 | convolution fusion | flops 273678336 | bytes 4268032 | tf_op jit(solution)/shard_map/while/body/eval_jaxpr/blh,blo->bho/dot_general | solution.py:23
  20.0 26.1 %all-gather.2.cloned.1.call-done = bf16[16384,128]{1,0:T(8,128)(2,1)} async-done(((bf16[4096,128]{1,0:T(8,128)(2,1)}), bf16[16384,128]{1,0:T(8,128)(2,1)}) %all-gather.2.cloned.1.call-update) | async-done | bytes 4194320 | tf_op jit(solution)/shard_map/all_gather | solution.py:47
  46.2 6.9 %fusion = f32[128,128]{1,0:T(8,128)} fusion(bf16[16384,128]{1,0:T(8,128)(2,1)} %all-gather.2.cloned.1.call-done, bf16[16,8,128,128]{3,2,1,0:T(8,128)(2,1)} %bitcast.5), kind=kOutput, calls=%fused_computation | convolution fusion | flops 536870912 | bytes 8454144 | tf_op jit(solution)/shard_map/while/body/eval_jaxpr/dot_general | solution.py:25
  53.0 0.0 all-reduce.2.cloned.1.call-update
  53.1 69.4 %all-reduce.2.cloned.1.call-done = f32[128,128]{1,0:T(8,128)} async-done(((f32[128,128]{1,0:T(8,128)}), f32[128,128]{1,0:T(8,128)}) %all-reduce.2.cloned.1.call-update) | async-done | bytes 65552 | tf_op jit(solution)/shard_map/psum | solution.py:50
  122.5 0.9 multiply_reduce_fusion
  123.5 1.6 %broadcast_divide_fusion = f32[128,128]{1,0:T(8,128)} fusion(f32[128,128]{1,0:T(8,128)} %all-reduce.2.cloned.1.call-done, f32[128]{0:T(128)S(1)} %add_sqrt_fusion), kind=kLoop, calls=%fused_computation.17 | loop fusion | flops 16384 | bytes 131584 | tf_op jit(solution)/shard_map/div | solution.py:36
  (1 shorter events, 0.0 us)
Async XLA Ops:
  6.5 39.6 %all-gather.2.cloned.1.call-start = ((), (), s32[]{:S(2)}) async-start(), calls=%async_computation | async-start | bytes 5242880 | tf_op jit(solution)/shard_map/all_gather | solution.py:47
  7.3 115.2 %all-reduce.2.cloned.1.call-start = ((), (), s32[]{:S(2)}) async-start(), calls=%async_computation.1 | async-start | bytes 131072 | tf_op jit(solution)/shard_map/psum | solution.py:50
Sparse Core Ops, SparseCore 0:
  8.9 37.2 all-gather.1
  53.2 69.2 all-reduce.1
where the time goes:
time: 132 us
  waiting for transfers between devices  96.3 us (73%)
  matrix products  17.7 us (13%)
  between operations  13.4 us (10%)
  other arithmetic  4.08 us (3%)
    psum x1, waiting for transfers between devices, on_device(): pooled = lax.psum(partial_value, 'rep')  69.4 us
    all_gather x1, waiting for transfers between devices, on_device(): lax.all_gather(item_table, 'rows', axis=0, tiled=True)  26.1 us
    dot_general x1, matrix products, one_block(): jnp.einsum('blh,blo->bho', high_hot, low_hot, preferred_element_type=jnp....  10.8 us
    dot_general x1, matrix products, one_block(): return jnp.dot(counts, piece, preferred_element_type=jnp.float32)  6.88 us
  transfers between devices with their start and end apart: 2, of which 2 were waited for; matrix products, arithmetic and copies ran while one was open for 10% of the time, Pallas kernels for 0%

commit v1 on v0

--- a/solution.py
+++ b/solution.py
@@ -47,7 +47,7 @@
         lax.all_gather(item_table, "rows", axis=0, tiled=True),
         group_base,
     )
-    pooled = lax.psum(partial_value, "rep")
+    pooled = jnp.sum(lax.all_gather(partial_value, "rep"), axis=0)
     return normalize(pooled)
 
 

time: 132 us -> 92 us (0.70)
  waiting for transfers between devices: 96.3 us -> 26.8 us
  blocking collectives: 0 us -> 31.6 us
  other arithmetic: 4.08 us -> 2.44 us
    psum x1 -> x0, waiting for transfers between devices: 69.4 us -> none  [on_device(): pooled = lax.psum(partial_value, 'rep')]
    all_gather x0 -> x1, blocking collectives: none -> 31.6 us  [on_device(): pooled = jnp.sum(lax.all_gather(partial_value, 'rep'), axis=0)]
  transfers between devices with their start and end apart: 2 -> 1, of which waited for: 2 -> 1; matrix products, arithmetic and copies ran while one was open for 10% -> 14% of each run, Pallas kernels for 0% -> 0%
where the time goes in v1:
time: 92 us; the launch traced here: 91.7 us
  blocking collectives  31.6 us (34%)
  waiting for transfers between devices  26.8 us (29%)
  matrix products  17.1 us (19%)
  between operations  13.4 us (15%)
  other arithmetic  2.44 us (3%)
    all_gather x1, blocking collectives, on_device(): pooled = jnp.sum(lax.all_gather(partial_value, 'rep'), axis=0)  31.6 us
    all_gather x1, waiting for transfers between devices, on_device(): lax.all_gather(item_table, 'rows', axis=0, tiled=True)  26.1 us
    dot_general x1, matrix products, one_block(): jnp.einsum('blh,blo->bho', high_hot, low_hot, preferred_element_type=jnp....  10.8 us
    dot_general x1, matrix products, one_block(): return jnp.dot(counts, piece, preferred_element_type=jnp.float32)  6.31 us
  transfers between devices with their start and end apart: 1, of which 1 were waited for; matrix products, arithmetic and copies ran while one was open for 14% of the time, Pallas kernels for 0%

profile of v1, /device:TPU:0, one launch (start us, length us, event | category | flops | bytes accessed | tf_op | source)
XLA Modules:
  0.0 91.7 jit_solution(13632765863746206246)
XLA Ops:
  6.5 0.0 all-gather.3.cloned.1.call-start
  6.5 0.7 all-gather.3.cloned.1.call-update
  7.3 0.8 add_select_fusion.1
  8.1 0.1 copy.4
  8.2 0.1 copy.5
  8.3 0.8 broadcast_compare_fusion
  9.0 0.1 copy.6
  9.1 10.8 %fusion.6 = bf16[128,128,128]{2,1,0:T(8,128)(2,1)} fusion(s32[128,64]{1,0:T(8,128)S(1)} %copy.5, s32[128,64]{1,0:T(8,128)S(1)} %copy.4, pred[128,64]{1,0:T(8,128)(4,1)S(1)} %copy.6), kind=kOutput, calls=%fused_computation.7 | convolution fusion | flops 273678336 | bytes 4268032 | tf_op jit(solution)/shard_map/while/body/eval_jaxpr/blh,blo->bho/dot_general | solution.py:23
  20.0 26.1 %all-gather.3.cloned.1.call-done = bf16[16384,128]{1,0:T(8,128)(2,1)} async-done(((bf16[4096,128]{1,0:T(8,128)(2,1)}), bf16[16384,128]{1,0:T(8,128)(2,1)}) %all-gather.3.cloned.1.call-update) | async-done | bytes 4194320 | tf_op jit(solution)/shard_map/all_gather | solution.py:47
  46.1 6.3 %fusion = f32[128,128]{1,0:T(8,128)S(1)} fusion(bf16[16384,128]{1,0:T(8,128)(2,1)} %all-gather.3.cloned.1.call-done, bf16[16,8,128,128]{3,2,1,0:T(8,128)(2,1)} %bitcast.7), kind=kOutput, calls=%fused_computation | convolution fusion | flops 536870912 | bytes 8454144 | tf_op jit(solution)/shard_map/while/body/eval_jaxpr/dot_general | solution.py:25
  52.4 31.6 %all-gather = f32[1024,128]{1,0:T(8,128)S(1)} all-gather(f32[128,128]{1,0:T(8,128)S(1)} %fusion), channel_id=2, replica_groups=mesh['rep'=8,'rows'=4] {'rep'}, dimensions={0}, use_global_device_ids=true | all-gather | bytes 589824 | tf_op jit(solution)/shard_map/all_gather | solution.py:50
  84.0 0.1 multiply_reduce_fusion
  84.2 0.7 broadcast_divide_fusion
  (2 shorter events, 0.0 us)
Async XLA Ops:
  6.5 39.6 %all-gather.3.cloned.1.call-start = ((), (), s32[]{:S(2)}) async-start(), calls=%async_computation | async-start | bytes 5242880 | tf_op jit(solution)/shard_map/all_gather | solution.py:47
Sparse Core Ops, SparseCore 0:
  8.9 37.1 all-gather.2

commit v2 on v0

--- a/solution.py
+++ b/solution.py
@@ -44,7 +44,9 @@
     partial_value = pool_rows(
         history_ids,
         history_mask,
-        lax.all_gather(item_table, "rows", axis=0, tiled=True),
+        jnp.concatenate(
+            lax.all_to_all(jnp.stack([item_table] * lax.axis_size("rows")), "rows", 0, 0), axis=0
+        ),
         group_base,
     )
     pooled = lax.psum(partial_value, "rep")

time: 132 us -> 151 us (1.14)
  waiting for transfers between devices: 96.3 us -> 108 us
  starting transfers between devices: 0.04 us -> 5.01 us
  local copies, waits for them, and re-layouts: 0.3 us -> 4.04 us
  other arithmetic: 4.08 us -> 2.56 us
    all_to_all x0 -> x1, waiting for transfers between devices: none -> 37.6 us  [on_device(): lax.all_to_all(jnp.stack([item_table] * lax.axis_size('rows')), 'rows', 0...]
    all_gather x1 -> x0, waiting for transfers between devices: 26.1 us -> none  [on_device(): lax.all_gather(item_table, 'rows', axis=0, tiled=True)]
    all_to_all x0 -> x1, starting transfers between devices: none -> 4.97 us  [on_device(): lax.all_to_all(jnp.stack([item_table] * lax.axis_size('rows')), 'rows', 0...]
    another operation x0 -> x1, local copies, waits for them, and re-layouts: none -> 3.74 us  [on_device(): jnp.stack([item_table] * lax.axis_size('rows'))]
  transfers between devices with their start and end apart: 2 -> 2, of which waited for: 2 -> 2; matrix products, arithmetic and copies ran while one was open for 10% -> 7% of each run, Pallas kernels for 0% -> 0%
where the time goes in v2:
time: 151 us
  waiting for transfers between devices  108 us (72%)
  matrix products  17.7 us (12%)
  between operations  13.5 us (9%)
  starting transfers between devices  5.01 us (3%)
  local copies, waits for them, and re-layouts  4.04 us (3%)
  other arithmetic  2.56 us (2%)
    psum x1, waiting for transfers between devices, on_device(): pooled = lax.psum(partial_value, 'rep')  70.5 us
    all_to_all x1, waiting for transfers between devices, on_device(): lax.all_to_all(jnp.stack([item_table] * lax.axis_size('rows')), 'rows', 0...  37.6 us
    dot_general x1, matrix products, one_block(): jnp.einsum('blh,blo->bho', high_hot, low_hot, preferred_element_type=jnp....  10.8 us
    dot_general x1, matrix products, one_block(): return jnp.dot(counts, piece, preferred_element_type=jnp.float32)  6.88 us
    all_to_all x1, starting transfers between devices, on_device(): lax.all_to_all(jnp.stack([item_table] * lax.axis_size('rows')), 'rows', 0...  4.97 us
    another operation x1, local copies, waits for them, and re-layouts, on_device(): jnp.stack([item_table] * lax.axis_size('rows'))  3.74 us
  transfers between devices with their start and end apart: 2, of which 2 were waited for; matrix products, arithmetic and copies ran while one was open for 7% of the time, Pallas kernels for 0%

profile of v2, /device:TPU:0, one launch (start us, length us, event | category | flops | bytes accessed | tf_op | source)
XLA Modules:
  0.0 150.9 jit_solution(2778348524605024095)
XLA Ops:
  6.5 3.7 %stack.2 = bf16[4,4096,128]{2,1,0:T(8,128)(2,1)} broadcast(bf16[4096,128]{1,0:T(8,128)(2,1)} %param.3), dimensions={1,2} | broadcast | bytes 5242880 | tf_op jit(solution)/shard_map/stack | solution.py:48
  10.3 0.0 copy-start
  10.3 0.0 copy-start.1
  10.3 5.0 %all-to-all-start = ((bf16[4,4096,128]{2,1,0:T(8,128)(2,1)}), bf16[4,4096,128]{2,1,0:T(8,128)(2,1)}, u32[]{:S(2)}, u32[]{:S(2)}) async-start(bf16[4,4096,128]{2,1,0:T(8,128)(2,1)} %stack.2), calls=%async_computation | async-start | bytes 8388608 | tf_op jit(solution)/shard_map/all_to_all | solution.py:48
  15.3 0.0 all-reduce.2.cloned.1.call-start
  15.3 0.0 copy-done
  15.4 0.1 copy.5
  15.5 0.1 copy.4
  15.6 0.0 copy-done.1
  15.6 0.1 copy.6
  15.7 10.8 %fusion.6 = bf16[128,128,128]{2,1,0:T(8,128)(2,1)} fusion(s32[128,64]{1,0:T(8,128)S(1)} %copy.5, s32[128,64]{1,0:T(8,128)S(1)} %copy.4, pred[128,64]{1,0:T(8,128)(4,1)S(1)} %copy.6), kind=kOutput, calls=%fused_computation.7 | convolution fusion | flops 273678336 | bytes 4268032 | tf_op jit(solution)/shard_map/while/body/eval_jaxpr/blh,blo->bho/dot_general | solution.py:23
  26.5 37.6 %all-to-all-done = bf16[4,4096,128]{2,1,0:T(8,128)(2,1)} async-done(((bf16[4,4096,128]{2,1,0:T(8,128)(2,1)}), bf16[4,4096,128]{2,1,0:T(8,128)(2,1)}, u32[]{:S(2)}, u32[]{:S(2)}) %all-to-all-start) | async-done | bytes 4194336 | tf_op jit(solution)/shard_map/all_to_all | solution.py:48
  64.1 6.9 %fusion = f32[128,128]{1,0:T(8,128)} fusion(bf16[16384,128]{1,0:T(8,128)(2,1)} %bitcast, bf16[16,8,128,128]{3,2,1,0:T(8,128)(2,1)} %bitcast.6), kind=kOutput, calls=%fused_computation | convolution fusion | flops 536870912 | bytes 8454144 | tf_op jit(solution)/shard_map/while/body/eval_jaxpr/dot_general | solution.py:25
  71.0 0.0 all-reduce.2.cloned.1.call-update
  71.1 70.5 %all-reduce.2.cloned.1.call-done = f32[128,128]{1,0:T(8,128)} async-done(((f32[128,128]{1,0:T(8,128)}), f32[128,128]{1,0:T(8,128)}) %all-reduce.2.cloned.1.call-update) | async-done | bytes 65552 | tf_op jit(solution)/shard_map/psum | solution.py:52
  141.5 0.9 multiply_reduce_fusion
  142.5 1.6 %broadcast_divide_fusion = f32[128,128]{1,0:T(8,128)} fusion(f32[128,128]{1,0:T(8,128)} %all-reduce.2.cloned.1.call-done, f32[128]{0:T(128)S(1)} %add_sqrt_fusion), kind=kLoop, calls=%fused_computation.17 | loop fusion | flops 16384 | bytes 131584 | tf_op jit(solution)/shard_map/div | solution.py:36
  (3 shorter events, 0.1 us)
Async XLA Ops:
  10.3 5.0 %copy-start = (s32[128,64]{0,1:T(8,128)S(1)}, s32[128,64]{0,1:T(8,128)}, u32[]{:S(2)}) copy-start(s32[128,64]{0,1:T(8,128)} %param.4) | copy-start | bytes 98308
  10.3 5.3 %copy-start.1 = (s32[128,64]{0,1:T(8,128)S(1)}, s32[128,64]{0,1:T(8,128)}, u32[]{:S(2)}) copy-start(s32[128,64]{0,1:T(8,128)} %param.5) | copy-start | bytes 98308
  10.3 53.9 %all-to-all-start = ((bf16[4,4096,128]{2,1,0:T(8,128)(2,1)}), bf16[4,4096,128]{2,1,0:T(8,128)(2,1)}, u32[]{:S(2)}, u32[]{:S(2)}) async-start(bf16[4,4096,128]{2,1,0:T(8,128)(2,1)} %stack.2), calls=%async_computation | async-start | bytes 8388608 | tf_op jit(solution)/shard_map/all_to_all | solution.py:48
  15.3 126.3 %all-reduce.2.cloned.1.call-start = ((), (), s32[]{:S(2)}) async-start(), calls=%async_computation.1 | async-start | bytes 131072 | tf_op jit(solution)/shard_map/psum | solution.py:52
Sparse Core Ops, SparseCore 0:
  71.2 70.3 all-reduce.1
